TPU v7x, 32 devices: a whole 2x2x4 slice. The times are simulated.
32 devices in a mesh: rows: 8 (over z, x), cols: 4 (over y, core).
Axes of the slice: x: 2, y: 2, z: 4, core: 2. Of those that a mesh axis runs over, the one named last changes fastest.
Arguments:
- vectors: bfloat16 [1024, 32768], P(None, 'rows'), may hold values from -0.4 to 0.4
- integrals: bfloat16 [2, 256, 32768], P(None, 'cols', 'rows'), may hold values from -8 to 72
- pivots: int32 [2, 256], replicated, may hold values from 0 to 32767, as said below
Outputs:
- new_vectors: float32 [2, 256, 32768], P(None, 'cols', 'rows')
Inputs may be any that keep to these rules, and one draw needn't show every extreme that they name: The 2 x 256 entries are distinct shell-pair rows. In each panel the rows of one index of rows (an aligned block of 4096) hold at most 64 pivots, and some block holds exactly 64.
All inputs are finite; a program needn't handle non-finite values.
Results may differ from a plain program's by a relative error of at most 0.00036.
Values may be sent and summed in bfloat16 or wider, within the bound.
No kernel may reach another device: no remote copies, remote signals or barrier semaphores. Data moves between devices by JAX's collectives and lax.ppermute only.
A program may use at most 64 MiB of HBM per device.

v0:
```python
import jax
import jax.numpy as jnp
from jax import lax
from jax.sharding import PartitionSpec as P

PW = 256
PANELS = 2


def select_matrix(row_count, targets):
    return (jnp.arange(row_count, dtype=jnp.int32)[:, None] == targets[None, :]).astype(
        jnp.bfloat16
    )


def transposed_product(left, right):
    return lax.dot_general(
        left, right, (((0,), (0,)), ((), ())), preferred_element_type=jnp.float32
    )


def solve_block(lower_factor, residual):
    return jax.scipy.linalg.solve_triangular(lower_factor, residual, lower=True)


def per_device(vectors, integrals, pivots):
    row_count = vectors.shape[1]
    block_cols = integrals.shape[1]
    owners = lax.axis_size("rows")
    owner_index = lax.axis_index("rows")
    owner_start = owner_index * row_count
    col_start = lax.axis_index("cols") * block_cols
    factors = [vectors]
    results = []
    for panel in range(PANELS):
        pivot_row = pivots[panel]
        local_targets = pivot_row - owner_start
        slot_count = 2 * PW // owners
        owner_of = pivot_row // row_count
        order = jnp.arange(PW, dtype=jnp.int32)
        earlier = (owner_of[None, :] == owner_of[:, None]) & (order[None, :] < order[:, None])
        slot_rank = jnp.sum(earlier.astype(jnp.int32), axis=1)
        mine = owner_of == owner_index
        slot_pick = (
            (slot_rank[:, None] == jnp.arange(slot_count, dtype=jnp.int32)[None, :]) & mine[:, None]
        ).astype(jnp.bfloat16)
        slot_select = jnp.dot(
            select_matrix(row_count, local_targets), slot_pick, preferred_element_type=jnp.float32
        ).astype(jnp.bfloat16)
        sending = jnp.concatenate(
            [
                jnp.dot(factor, slot_select, preferred_element_type=jnp.float32)
                for factor in factors
            ],
            axis=0,
        ).astype(jnp.bfloat16)
        targets = lax.dynamic_slice_in_dim(owner_of * slot_count + slot_rank, col_start, block_cols)
        receive_pick = select_matrix(owners * slot_count, targets)
        picked = jnp.dot(
            lax.all_gather(sending, "rows", axis=1, tiled=True),
            receive_pick,
            preferred_element_type=jnp.float32,
        ).astype(jnp.bfloat16)
        residual = integrals[panel].astype(jnp.float32)
        offset = 0
        for factor in factors:
            residual = residual - transposed_product(
                picked[offset : offset + factor.shape[0]], factor
            )
            offset = offset + factor.shape[0]
        every_pivot = select_matrix(row_count, local_targets).astype(jnp.float32)
        contribution = jnp.dot(residual, every_pivot, precision=lax.Precision.HIGHEST)
        placed = lax.dynamic_update_slice(
            jnp.zeros((PW, PW), jnp.float32), contribution, (col_start, 0)
        )
        block = lax.psum(placed, ("rows", "cols"))
        lower_factor = jnp.linalg.cholesky(0.5 * (block + block.T))
        whole = lax.all_gather(residual, "cols", axis=0, tiled=True)
        solved = solve_block(lower_factor, whole)
        fresh = lax.dynamic_slice_in_dim(solved, col_start, block_cols, 0)
        if panel + 1 < PANELS:
            factors.append(solved.astype(jnp.bfloat16))
        results.append(fresh)
    return jnp.stack(results)


def solution(mesh):
    placed = (P(None, "rows"), P(None, "cols", "rows"), P())
    return jax.shard_map(
        per_device, mesh=mesh, in_specs=placed, out_specs=P(None, "cols", "rows"), check_vma=False
    )
```

profile of v0, /device:TPU:0, one launch (start us, length us, event | category | flops | bytes accessed | tf_op | source)
XLA Modules:
  0.0 519.9 jit_solution(4560592978291593466)
XLA Ops:
  6.5 0.8 fusion.58
  7.5 7.5 %fusion.14 = bf16[1024,64]{0,1:T(8,128)(2,1)} fusion(bf16[1024,4096]{1,0:T(8,128)(2,1)} %param.6, s32[256]{0:T(256)S(1)} %bitcast.98, s32[256]{0:T(256)S(1)} %convert_reduce_fusion.1, pred[256]{0:T(512)(128)(4,1)S(1)} %get-tuple-element.65), kind=kOutput, calls=%fused_computation.36 | convolution fusion | flops 672497664 | bytes 8521984 | tf_op jit(solution)/shard_map/dot_general | solution.py:52
  15.2 43.0 %all-gather.5.cloned.1.call-done = bf16[1024,512]{0,1:T(8,128)(2,1)} async-done(((bf16[1024,64]{0,1:T(8,128)(2,1)}), bf16[1024,512]{0,1:T(8,128)(2,1)}) %all-gather.5.cloned.1.call-update) | async-done | bytes 1048592 | tf_op jit(solution)/shard_map/all_gather | solution.py:60
  58.2 5.9 %convolution_subtract_fusion.4 = f32[64,4096]{1,0:T(8,128)S(1)} fusion(bf16[1024,4096]{1,0:T(8,128)(2,1)} %param.6, bf16[1024,512]{0,1:T(8,128)(2,1)} %all-gather.5.cloned.1.call-done, bf16[2,64,4096]{2,1,0:T(8,128)(2,1)S(1)} %copy-done.6, s32[64]{0:T(128)S(1)} %dynamic_slice.12), kind=kOutput, calls=%fused_computation.12 | convolution fusion | flops 604602368 | bytes 11010304 | tf_op jit(solution)/shard_map/dot_general | solution.py:17
  64.1 1.7 fusion.15
  65.8 0.7 copy-done.8
  66.6 0.7 all-gather.7.cloned.1.call-update
  67.7 1.0 convolution_convert_fusion.1
  68.7 6.1 %fusion.13 = bf16[1024,64]{0,1:T(8,128)(2,1)S(1)} fusion(bf16[4096,64]{0,1:T(8,128)(2,1)S(1)} %convolution_convert_fusion.1, bf16[1024,4096]{1,0:T(8,128)(2,1)} %param.6), kind=kOutput, calls=%fused_computation.35 | convolution fusion | flops 536936448 | bytes 9043968 | tf_op jit(solution)/shard_map/dot_general | solution.py:52
  74.7 117.2 %all-reduce.4.cloned.1.call-done = f32[256,256]{1,0:T(8,128)} async-done(((f32[256,256]{1,0:T(8,128)}), f32[256,256]{1,0:T(8,128)}) %all-reduce.4.cloned.1.call-update) | async-done | bytes 262160 | tf_op jit(solution)/shard_map/psum | solution.py:76
  192.0 1.1 copy.9
  193.1 1.0 fusion.25
  194.2 11.7 %cholesky.130 = f32[128,128]{1,0:T(8,128)S(1)} custom-call(f32[128,128]{1,0:T(8,128)S(1)} %cholesky.194), custom_call_target="Cholesky" | custom-call | tf_op jit(solution)/shard_map/jit(cholesky)/cholesky | solution.py:77
  206.0 9.8 %custom-call.13 = f32[1,128,128]{1,2,0:T(8,128)S(1)} custom-call(f32[1,128,128]{2,1,0:T(8,128)S(1)} %get-tuple-element.54), custom_call_target="InvertDiagBlocksLowerTriangular" | custom-call | tf_op jit(solution)/shard_map/jit(cholesky)/cholesky | solution.py:77
  216.3 11.9 %cholesky.147 = f32[128,128]{1,0:T(8,128)S(1)} custom-call(f32[128,128]{1,0:T(8,128)S(1)} %convolution_subtract_fusion.6), custom_call_target="Cholesky" | custom-call | tf_op jit(solution)/shard_map/jit(cholesky)/cholesky | solution.py:77
  228.2 0.7 compare_reduce_fusion.3
  228.9 0.7 compare_reduce_fusion.2
  231.0 4.1 while.4
  231.0 0.6 fusion.79
  231.7 1.4 bitcast_dynamic-update-slice_fusion.4
  233.1 0.6 fusion.79
  233.7 1.4 bitcast_dynamic-update-slice_fusion.4
  235.1 19.7 %custom-call.14 = f32[2,128,128]{1,2,0:T(8,128)S(1)} custom-call(f32[2,128,128]{2,1,0:T(8,128)S(1)} %get-tuple-element.21), custom_call_target="InvertDiagBlocksLowerTriangular" | custom-call | tf_op jit(solution)/shard_map/jit(_solve_triangular)/triangular_solve | solution.py:23
  254.8 3.6 fusion.5
  258.5 1.9 convolution_subtract_fusion.1
  260.4 1.9 fusion.42
  262.4 0.8 convolution_convert_fusion.5
  263.7 0.7 pad_maximum_fusion.2
  264.6 40.9 %all-gather.9.cloned.1.call-done = bf16[1280,512]{0,1:T(8,128)(2,1)} async-done(((bf16[1280,64]{0,1:T(8,128)(2,1)}), bf16[1280,512]{0,1:T(8,128)(2,1)}) %all-gather.9.cloned.1.call-update) | async-done | bytes 1310736 | tf_op jit(solution)/shard_map/all_gather | solution.py:60
  305.5 1.7 convolution_convert_fusion.2
  307.2 5.1 convolution_subtract_fusion.3
  312.9 1.7 fusion.16
  314.6 0.7 copy-done.9
  316.0 124.8 %all-reduce.6.cloned.1.call-done = f32[256,256]{1,0:T(8,128)} async-done(((f32[256,256]{1,0:T(8,128)}), f32[256,256]{1,0:T(8,128)}) %all-reduce.6.cloned.1.call-update) | async-done | bytes 262160 | tf_op jit(solution)/shard_map/psum | solution.py:76
  440.9 1.1 copy.11
  441.9 1.0 bitcast_add_fusion.1
  443.3 11.7 %cholesky.164 = f32[128,128]{1,0:T(8,128)S(1)} custom-call(f32[128,128]{1,0:T(8,128)S(1)} %cholesky.197), custom_call_target="Cholesky" | custom-call | tf_op jit(solution)/shard_map/jit(cholesky)/cholesky | solution.py:77
  455.0 9.8 %custom-call.15 = f32[1,128,128]{1,2,0:T(8,128)S(1)} custom-call(f32[1,128,128]{2,1,0:T(8,128)S(1)} %get-tuple-element.50), custom_call_target="InvertDiagBlocksLowerTriangular" | custom-call | tf_op jit(solution)/shard_map/jit(cholesky)/cholesky | solution.py:77
  465.4 11.7 %cholesky.181 = f32[128,128]{1,0:T(8,128)S(1)} custom-call(f32[128,128]{1,0:T(8,128)S(1)} %convolution_subtract_fusion.5), custom_call_target="Cholesky" | custom-call | tf_op jit(solution)/shard_map/jit(cholesky)/cholesky | solution.py:77
  477.8 0.6 compare_reduce_fusion
  479.7 4.1 while.5
  480.5 1.4 bitcast_dynamic-update-slice_fusion.5
  482.5 1.4 bitcast_dynamic-update-slice_fusion.5
  483.9 19.7 %custom-call.16 = f32[2,128,128]{1,2,0:T(8,128)S(1)} custom-call(f32[2,128,128]{2,1,0:T(8,128)S(1)} %get-tuple-element.22), custom_call_target="InvertDiagBlocksLowerTriangular" | custom-call | tf_op jit(solution)/shard_map/jit(_solve_triangular)/triangular_solve | solution.py:23
  503.6 3.6 fusion.3
  507.2 1.9 convolution_subtract_fusion
  509.2 1.9 fusion.38
  511.3 1.5 pad_maximum_fusion.1
  (74 shorter events, 6.6 us)
Async XLA Ops:
  6.5 51.7 %all-gather.5.cloned.1.call-start = ((), (), s32[]{:S(2)}) async-start(), calls=%async_computation | async-start | bytes 1179648 | tf_op jit(solution)/shard_map/all_gather | solution.py:60
  7.5 50.7 %copy-start.6 = (bf16[2,64,4096]{2,1,0:T(8,128)(2,1)S(1)}, bf16[2,64,4096]{2,1,0:T(8,128)(2,1)}, u32[]{:S(2)}) copy-start(bf16[2,64,4096]{2,1,0:T(8,128)(2,1)} %param.7) | copy-start | bytes 3145732
  15.0 176.9 %all-reduce.4.cloned.1.call-start = ((), (), s32[]{:S(2)}) async-start(), calls=%async_computation.1 | async-start | bytes 524288 | tf_op jit(solution)/shard_map/psum | solution.py:76
  64.1 2.5 copy-start.5
  65.8 0.7 copy-start.8
  66.5 188.3 %all-gather.7.cloned.1.call-start = ((), (), s32[]{:S(2)}) async-start(), calls=%async_computation.2 | async-start | bytes 5242880 | tf_op jit(solution)/shard_map/all_gather | solution.py:78
  67.3 238.2 %all-gather.9.cloned.1.call-start = ((), (), s32[]{:S(2)}) async-start(), calls=%async_computation.3 | async-start | bytes 1474560 | tf_op jit(solution)/shard_map/all_gather | solution.py:60
  254.8 3.7 copy-start.2
  262.4 1.3 copy-start
  263.7 43.5 %copy-start.7 = (bf16[2,64,4096]{2,1,0:T(8,128)(2,1)S(1)}, bf16[2,64,4096]{2,1,0:T(8,128)(2,1)}, u32[]{:S(2)}) copy-start(bf16[2,64,4096]{2,1,0:T(8,128)(2,1)} %param.7) | copy-start | bytes 3145732
  264.4 176.4 %all-reduce.6.cloned.1.call-start = ((), (), s32[]{:S(2)}) async-start(), calls=%async_computation.4 | async-start | bytes 524288 | tf_op jit(solution)/shard_map/psum | solution.py:76
  307.2 5.2 copy-start.1
  312.9 2.9 copy-start.4
  314.6 0.7 copy-start.9
  315.3 188.3 %all-gather.11.cloned.1.call-start = ((), (), s32[]{:S(2)}) async-start(), calls=%async_computation.5 | async-start | bytes 5242880 | tf_op jit(solution)/shard_map/all_gather | solution.py:78
  503.6 3.7 copy-start.3
Sparse Core Ops, SparseCore 0:
  15.2 42.9 all-gather.4
  66.6 125.2 all-reduce.3
  193.5 33.7 all-gather.6
  264.5 40.8 all-gather.8
  315.4 125.3 all-reduce.5
  442.3 33.6 all-gather.10
where the time goes:
time: 525 us; the launch traced here: 520 us
  waiting for transfers between devices  327 us (62%)
  other arithmetic  115 us (22%)
  matrix products  47.8 us (9%)
  between operations  16.7 us (3%)
  local copies, waits for them, and re-layouts  12.8 us (2%)
    psum x2, waiting for transfers between devices, per_device(): block = lax.psum(placed, ('rows', 'cols'))  242 us
    all_gather x2, waiting for transfers between devices, per_device(): lax.all_gather(sending, 'rows', axis=1, tiled=True)  83.9 us
    another operation x14, other arithmetic, per_device(): lower_factor = jnp.linalg.cholesky(0.5 * (block + block.T))  69.4 us
    another operation x5, other arithmetic, solve_block(): return jax.scipy.linalg.solve_triangular(lower_factor, residual, lower=True)  39.4 us
    another operation x6, matrix products, solve_block(): return jax.scipy.linalg.solve_triangular(lower_factor, residual, lower=True)  15 us
    dot_general x3, matrix products, per_device(): jnp.dot(factor, slot_select, preferred_element_type=jnp.float32)  14.4 us
    dot_general x3, matrix products, transposed_product(): lax.dot_general(left, right, (((0,), (0,)), ((), ())), preferred_element_...  11.5 us
  transfers between devices with their start and end apart: 6, of which 4 were waited for; matrix products, arithmetic and copies ran while one was open for 25% of the time, Pallas kernels for 0%

commit v1 on v0

--- a/solution.py
+++ b/solution.py
@@ -73,7 +73,7 @@
         placed = lax.dynamic_update_slice(
             jnp.zeros((PW, PW), jnp.float32), contribution, (col_start, 0)
         )
-        block = lax.psum(placed, ("rows", "cols"))
+        block = jnp.sum(lax.all_gather(placed, ("rows", "cols")), axis=0)
         lower_factor = jnp.linalg.cholesky(0.5 * (block + block.T))
         whole = lax.all_gather(residual, "cols", axis=0, tiled=True)
         solved = solve_block(lower_factor, whole)

time: 525 us -> 429 us (0.82)
  waiting for transfers between devices: 327 us -> 228 us
  other arithmetic: 115 us -> 121 us
    psum x2 -> x0, waiting for transfers between devices: 242 us -> none  [per_device(): block = lax.psum(placed, ('rows', 'cols'))]
    all_gather x0 -> x2, waiting for transfers between devices: none -> 143 us  [per_device(): block = jnp.sum(lax.all_gather(placed, ('rows', 'cols')), axis=0)]
    reduce_sum x0 -> x2, other arithmetic: none -> 7.86 us  [per_device(): block = jnp.sum(lax.all_gather(placed, ('rows', 'cols')), axis=0)]
  transfers between devices with their start and end apart: 6 -> 6, of which waited for: 4 -> 4; matrix products, arithmetic and copies ran while one was open for 25% -> 32% of each run, Pallas kernels for 0% -> 0%
where the time goes in v1:
time: 429 us; the launch traced here: 424 us
  waiting for transfers between devices  228 us (53%)
  other arithmetic  121 us (28%)
  matrix products  47.6 us (11%)
  between operations  16.7 us (4%)
  local copies, waits for them, and re-layouts  10.5 us (2%)
    all_gather x2, waiting for transfers between devices, per_device(): block = jnp.sum(lax.all_gather(placed, ('rows', 'cols')), axis=0)  143 us
    all_gather x2, waiting for transfers between devices, per_device(): lax.all_gather(sending, 'rows', axis=1, tiled=True)  83.5 us
    another operation x14, other arithmetic, per_device(): lower_factor = jnp.linalg.cholesky(0.5 * (block + block.T))  69.6 us
    another operation x5, other arithmetic, solve_block(): return jax.scipy.linalg.solve_triangular(lower_factor, residual, lower=True)  39.4 us
    another operation x6, matrix products, solve_block(): return jax.scipy.linalg.solve_triangular(lower_factor, residual, lower=True)  15 us
    dot_general x3, matrix products, per_device(): jnp.dot(factor, slot_select, preferred_element_type=jnp.float32)  14.5 us
    dot_general x3, matrix products, transposed_product(): lax.dot_general(left, right, (((0,), (0,)), ((), ())), preferred_element_...  11.2 us
  transfers between devices with their start and end apart: 6, of which 4 were waited for; matrix products, arithmetic and copies ran while one was open for 32% of the time, Pallas kernels for 0%

profile of v1, /device:TPU:0, one launch (start us, length us, event | category | flops | bytes accessed | tf_op | source)
XLA Modules:
  0.0 424.1 jit_solution(181477910736636313)
XLA Ops:
  6.5 0.8 fusion.61
  7.5 7.6 %fusion.14 = bf16[1024,64]{0,1:T(8,128)(2,1)} fusion(bf16[1024,4096]{1,0:T(8,128)(2,1)} %param.6, s32[256]{0:T(256)S(1)} %bitcast.108, s32[256]{0:T(256)S(1)} %convert_reduce_fusion.1, pred[256]{0:T(512)(128)(4,1)S(1)} %get-tuple-element.65), kind=kOutput, calls=%fused_computation.36 | convolution fusion | flops 672497664 | bytes 8521984 | tf_op jit(solution)/shard_map/dot_general | solution.py:52
  15.3 43.0 %all-gather.7.cloned.1.call-done = bf16[1024,512]{0,1:T(8,128)(2,1)} async-done(((bf16[1024,64]{0,1:T(8,128)(2,1)}), bf16[1024,512]{0,1:T(8,128)(2,1)}) %all-gather.7.cloned.1.call-update) | async-done | bytes 1048592 | tf_op jit(solution)/shard_map/all_gather | solution.py:60
  58.4 5.6 %convolution_subtract_fusion.4 = f32[64,4096]{1,0:T(8,128)S(1)} fusion(bf16[1024,4096]{1,0:T(8,128)(2,1)} %param.6, bf16[1024,512]{0,1:T(8,128)(2,1)} %all-gather.7.cloned.1.call-done, bf16[2,64,4096]{2,1,0:T(8,128)(2,1)S(1)} %copy-done.6, s32[64]{0:T(128)S(1)} %dynamic_slice.12), kind=kOutput, calls=%fused_computation.11 | convolution fusion | flops 604602368 | bytes 11010304 | tf_op jit(solution)/shard_map/dot_general | solution.py:17
  63.9 1.7 fusion.16
  65.6 0.7 copy-done.8
  66.4 0.7 all-gather.11.cloned.1.call-update
  67.5 1.0 convolution_convert_fusion
  68.5 6.0 %fusion.13 = bf16[1024,64]{0,1:T(8,128)(2,1)S(1)} fusion(bf16[4096,64]{0,1:T(8,128)(2,1)S(1)} %convolution_convert_fusion, bf16[1024,4096]{1,0:T(8,128)(2,1)} %param.6), kind=kOutput, calls=%fused_computation.35 | convolution fusion | flops 536936448 | bytes 9043968 | tf_op jit(solution)/shard_map/dot_general | solution.py:52
  74.5 67.8 %all-gather.9.cloned.1.call-done = f32[32,256,256]{2,1,0:T(8,128)} async-done(((f32[1,256,256]{2,1,0:T(8,128)}), f32[32,256,256]{2,1,0:T(8,128)}) %all-gather.9.cloned.1.call-update) | async-done | bytes 8388624 | tf_op jit(solution)/shard_map/all_gather | solution.py:76
  142.3 3.9 reduce_sum.37
  146.6 11.7 %cholesky.130 = f32[128,128]{1,0:T(8,128)S(1)} custom-call(f32[128,128]{1,0:T(8,128)S(1)} %cholesky.194), custom_call_target="Cholesky" | custom-call | tf_op jit(solution)/shard_map/jit(cholesky)/cholesky | solution.py:77
  158.3 9.8 %custom-call.13 = f32[1,128,128]{1,2,0:T(8,128)S(1)} custom-call(f32[1,128,128]{2,1,0:T(8,128)S(1)} %get-tuple-element.54), custom_call_target="InvertDiagBlocksLowerTriangular" | custom-call | tf_op jit(solution)/shard_map/jit(cholesky)/cholesky | solution.py:77
  168.7 12.1 %cholesky.147 = f32[128,128]{1,0:T(8,128)S(1)} custom-call(f32[128,128]{1,0:T(8,128)S(1)} %convolution_subtract_fusion.6), custom_call_target="Cholesky" | custom-call | tf_op jit(solution)/shard_map/jit(cholesky)/cholesky | solution.py:77
  180.8 0.7 compare_reduce_fusion.3
  181.5 0.6 compare_reduce_fusion.2
  183.4 3.8 while.4
  183.4 0.6 fusion.82
  184.0 1.3 bitcast_dynamic-update-slice_fusion.4
  185.3 0.6 fusion.82
  185.9 1.3 bitcast_dynamic-update-slice_fusion.4
  187.2 19.7 %custom-call.14 = f32[2,128,128]{1,2,0:T(8,128)S(1)} custom-call(f32[2,128,128]{2,1,0:T(8,128)S(1)} %get-tuple-element.21), custom_call_target="InvertDiagBlocksLowerTriangular" | custom-call | tf_op jit(solution)/shard_map/jit(_solve_triangular)/triangular_solve | solution.py:23
  206.9 3.6 fusion.5
  210.5 1.9 convolution_subtract_fusion.1
  212.5 1.9 fusion.45
  214.4 0.8 convolution_convert_fusion.5
  215.7 0.7 pad_maximum_fusion.2
  216.6 40.5 %all-gather.13.cloned.1.call-done = bf16[1280,512]{0,1:T(8,128)(2,1)} async-done(((bf16[1280,64]{0,1:T(8,128)(2,1)}), bf16[1280,512]{0,1:T(8,128)(2,1)}) %all-gather.13.cloned.1.call-update) | async-done | bytes 1310736 | tf_op jit(solution)/shard_map/all_gather | solution.py:60
  257.1 1.7 convolution_convert_fusion.2
  258.8 5.1 %convolution_subtract_fusion.3 = f32[64,4096]{1,0:T(8,128)S(1)} fusion(bf16[1024,4096]{1,0:T(8,128)(2,1)} %param.6, bf16[2,64,4096]{2,1,0:T(8,128)(2,1)S(1)} %copy-done.7, bf16[1280,64]{0,1:T(8,128)(2,1)S(1)} %convolution_convert_fusion.2), kind=kOutput, calls=%fused_computation.10 | convolution fusion | flops 537395200 | bytes 10092544 | tf_op jit(solution)/shard_map/dot_general | solution.py:17
  264.5 1.7 fusion.18
  266.2 0.7 copy-done.9
  267.6 75.3 %all-gather.15.cloned.1.call-done = f32[32,256,256]{2,1,0:T(8,128)} async-done(((f32[1,256,256]{2,1,0:T(8,128)}), f32[32,256,256]{2,1,0:T(8,128)}) %all-gather.15.cloned.1.call-update) | async-done | bytes 8388624 | tf_op jit(solution)/shard_map/all_gather | solution.py:76
  342.9 3.9 reduce_sum.39
  347.2 11.7 %cholesky.164 = f32[128,128]{1,0:T(8,128)S(1)} custom-call(f32[128,128]{1,0:T(8,128)S(1)} %cholesky.197), custom_call_target="Cholesky" | custom-call | tf_op jit(solution)/shard_map/jit(cholesky)/cholesky | solution.py:77
  359.0 9.8 %custom-call.15 = f32[1,128,128]{1,2,0:T(8,128)S(1)} custom-call(f32[1,128,128]{2,1,0:T(8,128)S(1)} %get-tuple-element.50), custom_call_target="InvertDiagBlocksLowerTriangular" | custom-call | tf_op jit(solution)/shard_map/jit(cholesky)/cholesky | solution.py:77
  369.3 11.7 %cholesky.181 = f32[128,128]{1,0:T(8,128)S(1)} custom-call(f32[128,128]{1,0:T(8,128)S(1)} %convolution_subtract_fusion.5), custom_call_target="Cholesky" | custom-call | tf_op jit(solution)/shard_map/jit(cholesky)/cholesky | solution.py:77
  381.0 0.6 compare_reduce_fusion.1
  381.7 0.7 compare_reduce_fusion
  383.8 4.3 %while.5 = (s32[]{:T(128)}, f32[256,256]{1,0:T(8,128)S(1)}, s32[2,2]{1,0:T(2,128)S(1)}, f32[2,128,128]{2,1,0:T(8,128)S(1)}, s32[]{:T(128)}) while((s32[]{:T(128)}, f32[256,256]{1,0:T(8,128)S(1)}, s32[2,2]{1,0:T(2,128)S(1)}, f32[2,128,128]{2,1,0:T(8,128)S(1)}, s32[]{:T(128)}) %tuple.69), condition=%wide.while_cond.clone, body=%wide.while_body.clone.sunk | while | flops 2 | bytes 131189 | solution.py:23
  384.0 0.6 fusion.83
  384.6 1.4 bitcast_dynamic-update-slice_fusion.5
  386.6 1.4 bitcast_dynamic-update-slice_fusion.5
  388.1 19.7 %custom-call.16 = f32[2,128,128]{1,2,0:T(8,128)S(1)} custom-call(f32[2,128,128]{2,1,0:T(8,128)S(1)} %get-tuple-element.22), custom_call_target="InvertDiagBlocksLowerTriangular" | custom-call | tf_op jit(solution)/shard_map/jit(_solve_triangular)/triangular_solve | solution.py:23
  407.8 3.6 fusion.3
  411.4 1.9 convolution_subtract_fusion
  413.4 1.9 fusion.41
  415.5 1.5 pad_maximum_fusion.1
  (74 shorter events, 5.6 us)
Async XLA Ops:
  6.5 51.8 %all-gather.7.cloned.1.call-start = ((), (), s32[]{:S(2)}) async-start(), calls=%async_computation | async-start | bytes 1179648 | tf_op jit(solution)/shard_map/all_gather | solution.py:60
  7.5 50.8 %copy-start.6 = (bf16[2,64,4096]{2,1,0:T(8,128)(2,1)S(1)}, bf16[2,64,4096]{2,1,0:T(8,128)(2,1)}, u32[]{:S(2)}) copy-start(bf16[2,64,4096]{2,1,0:T(8,128)(2,1)} %param.7) | copy-start | bytes 3145732
  15.2 127.1 %all-gather.9.cloned.1.call-start = ((), (), s32[]{:S(2)}) async-start(), calls=%async_computation.1 | async-start | bytes 8650752 | tf_op jit(solution)/shard_map/all_gather | solution.py:76
  63.9 2.5 copy-start.5
  65.6 0.7 copy-start.8
  66.4 140.5 %all-gather.11.cloned.1.call-start = ((), (), s32[]{:S(2)}) async-start(), calls=%async_computation.2 | async-start | bytes 5242880 | tf_op jit(solution)/shard_map/all_gather | solution.py:78
  67.1 190.0 %all-gather.13.cloned.1.call-start = ((), (), s32[]{:S(2)}) async-start(), calls=%async_computation.3 | async-start | bytes 1474560 | tf_op jit(solution)/shard_map/all_gather | solution.py:60
  206.9 3.7 copy-start.2
  214.4 1.3 copy-start
  215.7 43.0 %copy-start.7 = (bf16[2,64,4096]{2,1,0:T(8,128)(2,1)S(1)}, bf16[2,64,4096]{2,1,0:T(8,128)(2,1)}, u32[]{:S(2)}) copy-start(bf16[2,64,4096]{2,1,0:T(8,128)(2,1)} %param.7) | copy-start | bytes 3145732
  216.5 126.5 %all-gather.15.cloned.1.call-start = ((), (), s32[]{:S(2)}) async-start(), calls=%async_computation.4 | async-start | bytes 8650752 | tf_op jit(solution)/shard_map/all_gather | solution.py:76
  258.8 5.2 %copy-start.1 = (f32[128,4096]{1,0:T(8,128)S(1)}, f32[128,4096]{1,0:T(8,128)}, u32[]{:S(2)}) copy-start(f32[128,4096]{1,0:T(8,128)} %copy-done) | copy-start | bytes 6291460
  264.4 2.7 copy-start.4
  266.2 0.7 copy-start.9
  266.9 140.9 %all-gather.17.cloned.1.call-start = ((), (), s32[]{:S(2)}) async-start(), calls=%async_computation.5 | async-start | bytes 5242880 | tf_op jit(solution)/shard_map/all_gather | solution.py:78
  407.8 3.7 copy-start.3
Sparse Core Ops, SparseCore 0:
  15.3 42.9 all-gather.6
  66.5 75.7 all-gather.8
  143.9 33.1 all-gather.10
  216.6 40.4 all-gather.12
  267.0 75.8 all-gather.14
  344.3 33.2 all-gather.16
